TPU v7x, 256 devices: a whole 4x4x8 slice. The times are simulated.
256 devices in a mesh: turn: 8 (over y, core), blk: 16 (over x_lo, z), strip: 2 (over x_hi).
Axes of the slice: x: 4 (x_hi: 2, x_lo: 2; x = x_hi * 2 + x_lo), y: 4, z: 8, core: 2. Of those that a mesh axis runs over, the one named last changes fastest.
Arguments:
- echoes: bfloat16 [2, 2048, 32768], P(None, 'blk', ('turn', 'strip')), may hold values from -6 to 6
- filters: bfloat16 [2, 32, 32768], P(None, 'blk'), may hold values from -6 to 6
- slab_index: int32 [2048], P(('blk', 'turn')), may hold values from 0 to 31
- shifts: int32 [2048], P(('blk', 'turn')), may hold values from 0 to 32767
Outputs:
- focused: float32 [2, 2048, 32768], P(None, ('blk', 'turn'), 'strip')
All inputs are finite; a program needn't handle non-finite values.
Results may differ from a plain program's by a relative error of at most 0.0003.
Values may be sent and summed in bfloat16 or wider, within the bound.
A program may use at most 128 MiB of HBM per device.

v0:
```python
import functools
import math

import numpy as np
import jax
import jax.numpy as jnp
from jax import lax
from jax.experimental import pallas as pl
from jax.experimental.pallas import tpu as pltpu
from jax.sharding import PartitionSpec as P

N = 32768
f32, bf16 = jnp.float32, jnp.bfloat16
MESH = pl.DeviceIdType.MESH

def cis(phase, length, sign):
    ang = (np.asarray(phase, np.int64) % length).astype(np.float64) * (2 * np.pi / length)
    return np.cos(ang), sign * np.sin(ang)

def halves(mat):
    hi = mat.astype(np.float32).astype(bf16)
    lo = (mat - hi.astype(np.float64)).astype(np.float32).astype(bf16)
    return hi, lo

def tables():
    lane = np.arange(128)
    c, s = cis(np.outer(lane, lane), 128, -1)
    fwd = np.block([[c, s], [-s, c]])
    inv = np.block([[c, -s], [s, c]]) / N
    mats = np.stack([*halves(fwd), *halves(inv)])
    tile = np.arange(256)
    tw = np.stack(cis(np.outer(tile, lane), N, -1)).astype(np.float32)
    ij = np.outer(np.arange(16), np.arange(16)).reshape(256, 1) * np.ones((1, 128), np.int64)
    ct = np.stack(cis(ij, 256, -1)).astype(np.float32)
    return mats, np.concatenate([tw, ct])

R2 = math.sqrt(0.5)
C1, S1 = math.cos(math.pi / 8), math.sin(math.pi / 8)

def cadd(a, b): return (a[0] + b[0], a[1] + b[1])
def csub(a, b): return (a[0] - b[0], a[1] - b[1])

def turn16(a, p, sign):
    p = (sign * p) % 16
    q, r = divmod(p, 4)
    x, y = a
    if r == 2:
        x, y = ((x - y) * R2, (x + y) * R2)
    elif r:
        c, s = (C1, S1) if r == 1 else (S1, C1)
        x, y = (x * c - y * s, x * s + y * c)
    return [(x, y), (-y, x), (-x, -y), (y, -x)][q]

def fold4(a, b, c, d, sign):
    e, f, g, h = cadd(a, c), csub(a, c), cadd(b, d), csub(b, d)
    if sign > 0:
        t, u = (f[0] - h[1], f[1] + h[0]), (f[0] + h[1], f[1] - h[0])
    else:
        t, u = (f[0] + h[1], f[1] - h[0]), (f[0] - h[1], f[1] + h[0])
    return cadd(e, g), t, csub(e, g), u

def dft16(v, sign):
    cols = [fold4(v[b], v[b + 4], v[b + 8], v[b + 12], sign) for b in range(4)]
    out = [None] * 16
    for a in range(4):
        o = fold4(*[turn16(cols[b][a], a * b, sign) for b in range(4)], sign)
        for c in range(4):
            out[a + 4 * c] = o[c]
    return out

def dft8(v, sign):
    even = fold4(v[0], v[2], v[4], v[6], sign)
    odd = fold4(v[1], v[3], v[5], v[7], sign)
    odd = [turn16(o, 2 * i, sign) for i, o in enumerate(odd)]
    return [cadd(e, o) for e, o in zip(even, odd)] + [csub(e, o) for e, o in zip(even, odd)]

def half16(v, sign, flip):
    even = dft8(v[0::2], sign)
    odd = dft8([(flip * a, flip * b) for a, b in v[1::2]], sign)
    return [cadd(e, turn16(o, i, sign)) for i, (e, o) in enumerate(zip(even, odd))]

def cmul(a, c, s): return (a[0] * c - a[1] * s, a[0] * s + a[1] * c)
def cmulc(a, c, s): return (a[0] * c + a[1] * s, a[1] * c - a[0] * s)

def split(x):
    hi = x.astype(bf16)
    return hi, (x - hi.astype(f32)).astype(bf16)

def stage_j(xs, y, tab):
    def body(m1, _):
        lanes = pl.ds(pl.multiple_of(m1 * 128, 128), 128)
        v = [(xs[j, 0, :, lanes].astype(f32), xs[j, 1, :, lanes].astype(f32)) for j in range(16)]
        for k0, a in enumerate(dft16(v, -1)):
            if k0:
                row = pl.ds(m1 * 16 + k0, 1)
                a = cmul(a, tab[2, row, :], tab[3, row, :])
            y[0, k0 * 16 + m1], y[1, k0 * 16 + m1] = a
        return 0
    lax.fori_loop(0, 16, body, 0)

def put_pair(hi_ref, lo_ref, row, a, b):
    rows = pl.ds(pl.multiple_of(row, 16), 16)
    for part, lanes in ((0, slice(0, 128)), (1, slice(128, 256))):
        hi, lo = split(jnp.concatenate([a[part], b[part]], axis=0))
        hi_ref[rows, lanes] = hi
        lo_ref[rows, lanes] = lo

def stage_m(y, hi_ref, lo_ref, tab):
    def body(k0, _):
        out = dft16([(y[0, k0 * 16 + m1], y[1, k0 * 16 + m1]) for m1 in range(16)], -1)
        out = [cmul(a, tab[0, pl.ds(k0 + 16 * k1, 1), :], tab[1, pl.ds(k0 + 16 * k1, 1), :]) for k1, a in enumerate(out)]
        for k1 in range(0, 16, 2):
            put_pair(hi_ref, lo_ref, k0 * 128 + k1 * 8, out[k1], out[k1 + 1])
        return 0
    lax.fori_loop(0, 16, body, 0)

def dot3(hi, lo, whi, wlo):
    d = functools.partial(jnp.dot, preferred_element_type=f32)
    return d(hi, whi) + d(lo, whi) + d(hi, wlo)

def mid(hi_ref, lo_ref, resp, mats, chunk=512):
    def body(i, _):
        rows = pl.ds(pl.multiple_of(i * chunk, chunk), chunk)
        s = dot3(hi_ref[rows, :], lo_ref[rows, :], mats[0], mats[1])
        p = cmul((s[:, :128], s[:, 128:]), resp[0, rows, :], resp[1, rows, :])
        for part, lanes in ((0, slice(0, 128)), (1, slice(128, 256))):
            hi, lo = split(p[part])
            hi_ref[rows, lanes] = hi
            lo_ref[rows, lanes] = lo
        return 0
    lax.fori_loop(0, 2048 // chunk, body, 0)

def back(hi_ref, lo_ref, q, mats, chunk=512):
    def body(i, _):
        rows = pl.ds(pl.multiple_of(i * chunk, chunk), chunk)
        q[rows, :] = dot3(hi_ref[rows, :], lo_ref[rows, :], mats[2], mats[3])
        return 0
    lax.fori_loop(0, 2048 // chunk, body, 0)

def stage_k1(q, y, tab):
    def body(k0, _):
        v = []
        for k1 in range(16):
            rows = pl.ds(pl.multiple_of(k0 * 128 + k1 * 8, 8), 8)
            row = pl.ds(k0 + 16 * k1, 1)
            v.append(cmulc((q[rows, 0:128], q[rows, 128:256]), tab[0, row, :], tab[1, row, :]))
        for m1, a in enumerate(dft16(v, 1)):
            y[0, k0 * 16 + m1], y[1, k0 * 16 + m1] = a
        return 0
    lax.fori_loop(0, 16, body, 0)

def stage_k0(y, out, tab, flip, g):
    def body(m1, _):
        v = []
        for k0 in range(16):
            a = (y[0, k0 * 16 + m1], y[1, k0 * 16 + m1])
            if k0:
                row = pl.ds(m1 * 16 + k0, 1)
                a = cmulc(a, tab[2, row, :], tab[3, row, :])
            v.append(a)
        for j, a in enumerate(half16(v, 1, flip)):
            lanes = pl.ds(pl.multiple_of(j * 2048 + m1 * 128, 128), 128)
            out[0, 8 * g:8 * g + 8, lanes], out[1, 8 * g:8 * g + 8, lanes] = a
        return 0
    lax.fori_loop(0, 16, body, 0)

def phase(idx):
    idx = (idx & (N - 1))
    idx = jnp.where(idx >= N // 2, idx - N, idx)
    ang = idx.astype(f32) * (2 * math.pi / N)
    return jnp.cos(ang), -jnp.sin(ang)

def response(bank, slabs, shifts, resp):
    sub = lax.broadcasted_iota(jnp.int32, (8, 128), 0)
    lane = lax.broadcasted_iota(jnp.int32, (8, 128), 1)
    for g in range(2):
        def body(r, _):
            sl = slabs[8 * g + r]
            sh = shifts[8 * g + r]
            e = [phase((16 * (sub + 8 * h) + 256 * lane) * sh) for h in range(2)]
            w = phase(jnp.full((8, 128), 1, jnp.int32) * sh)
            for i in range(16):
                hr = bank[0, sl, 16 * i:16 * i + 16, :].astype(f32)
                hi = bank[1, sl, 16 * i:16 * i + 16, :].astype(f32)
                for h in range(2):
                    o = cmul((hr[8 * h:8 * h + 8], hi[8 * h:8 * h + 8]), *e[h])
                    rows = pl.ds((16 * i + 8 * h) * 8 + r, 8, stride=8)
                    resp[g, 0, rows, :] = o[0]
                    resp[g, 1, rows, :] = o[1]
                if i < 15:
                    e = [cmul(x, *w) for x in e]
            return 0
        lax.fori_loop(0, 8, body, 0)


def place_filters(raw, lines, turned, bank, part, chunk):
    def spread(i, _):
        lanes = pl.ds(pl.multiple_of(i * 2048, 2048), 2048)
        block = raw[:, lanes].astype(f32)
        for t in range(16):
            for slab in range(2):
                lines[slab, pl.ds(i * 16 + t, 1), :] = block[slab:slab + 1, 128 * t:128 * t + 128]
        return 0
    lax.fori_loop(0, 16, spread, 0)
    for slab in range(2):
        for h in range(2):
            flat = jnp.transpose(lines[slab, pl.ds(h, 128, stride=2), :])
            for b in range(8):
                turned[slab, pl.ds(8 * h + b, 16, stride=16), :] = flat[16 * b:16 * b + 16]
        bank[part, 2 * chunk + slab] = turned[slab].astype(bf16)


def kernel(
    echoes, filters, slabs, shifts, mats_h, tab_h, out_h,
    xs, est, bank, raw, lines, turned, mats, tab, y, ahi, alo, q, resp, out,
    loc, es, er, fs, fr, zs, zr, cs, cr,
):
    t, b, s = (lax.axis_index(n) for n in ("turn", "blk", "strip"))
    yy, core = t // 2, t % 2
    xlo, z = b // 8, b % 8
    xx = 2 * s + xlo

    def at_y(dy, dc):
        return (((yy + dy) % 4) * 2 + (core + dc) % 2, b, s)

    def at_x(d):
        x = (xx + d) % 4
        return (t, (x % 2) * 8 + z, x // 2)

    def at_z(d):
        return (t, xlo * 8 + (z + d) % 8, s)

    mate, twin = at_y(0, 1), (t, b, 1 - s)
    peers = [at_y(dy, dc) for dy, dc in ((0, 1), (1, 0), (3, 0), (1, 1), (3, 1), (2, 0), (2, 1))]

    barrier = pltpu.get_barrier_semaphore()
    known = peers + [twin, at_x(1), at_x(3), at_z(1), at_z(7)]
    for d in known:
        pl.semaphore_signal(barrier, inc=1, device_id=d, device_id_type=MESH)

    mine = 2 * t + s
    local = [
        pltpu.make_async_copy(filters.at[core], raw, loc.at[0]),
        pltpu.make_async_copy(echoes, est, loc.at[1]),
        pltpu.make_async_copy(echoes.at[:, t, 0], xs.at[0, mine], loc.at[2]),
        pltpu.make_async_copy(echoes.at[:, t, 1], xs.at[1, mine], loc.at[3]),
        pltpu.make_async_copy(mats_h, mats, loc.at[4]),
        pltpu.make_async_copy(tab_h, tab, loc.at[5]),
    ]
    for c in local:
        c.start()
    local[0].wait()
    place_filters(raw, lines, turned, bank, core, b)
    for c in local[1:]:
        c.wait()
    pl.semaphore_wait(barrier, len(known))

    sent = []

    def send(src, dst, ssem, rsem, device):
        c = pltpu.make_async_remote_copy(
            src, dst, ssem, rsem, device_id=device, device_id_type=MESH
        )
        c.start()
        sent.append(c)

    def arrived(ref, ssem, rsem):
        pltpu.make_async_remote_copy(
            ref, ref, ssem, rsem, device_id=twin, device_id_type=MESH
        ).wait_recv()

    def slot(device):
        return 2 * device[0] + s

    def forward(g, j):
        ref = xs.at[g, j]
        send(ref, ref, es.at[g, j], er.at[g, j], twin)

    def echo(g, device):
        j = slot(device)
        arrived(xs.at[g, j], es.at[g, j], er.at[g, j])
        forward(g, j)

    def chunk(u, d):
        side = xlo if u == 0 else 1 - xlo
        return 2 * (side * 8 + (z + d) % 8)

    def piece(u, d, hop, way):
        start = chunk(u, d)
        if hop == 4:
            return bank.at[core, pl.ds(start + way, 1)]
        return bank.at[core, pl.ds(start, 2)]

    def over_z(u, hop, way):
        d = (1 - hop) if way == 0 else (hop - 1)
        ref = piece(u, d % 8, hop, way)
        send(ref, ref, zs.at[way, hop - 1, u], zr.at[way, hop - 1, u], at_z(1 if way == 0 else 7))

    def over_core(ref, n):
        send(ref, ref, cs.at[n], cr.at[n], mate)

    def relay(u, hop):
        for way in range(2):
            d = (-hop if way == 0 else hop) % 8
            ref = piece(u, d, hop, way)
            arrived(ref, zs.at[way, hop - 1, u], zr.at[way, hop - 1, u])
            if hop < 4:
                over_z(u, hop + 1, way)
            n = 2 + (hop - 1) * 4 + 2 * u + way
            over_core(ref, n)

    own = bank.at[core, pl.ds(2 * b, 2)]
    for i, d in ((0, 1), (1, 3)):
        ref = bank.at[core, pl.ds(2 * b + i, 1)]
        send(ref, ref, fs.at[i], fr.at[i], at_x(d))
    over_z(0, 1, 0)
    over_z(0, 1, 1)
    for g in range(2):
        for k, d in enumerate(peers):
            send(est.at[:, d[0], g], xs.at[g, mine], loc.at[8 + 8 * g + k], er.at[g, mine], d)
        forward(g, mine)
    over_core(own, 0)

    echo(0, peers[0])
    for i in range(2):
        arrived(bank.at[core, pl.ds(chunk(1, 0) + i, 1)], fs.at[i], fr.at[i])
    over_z(1, 1, 0)
    over_z(1, 1, 1)
    over_core(bank.at[core, pl.ds(chunk(1, 0), 2)], 1)
    for d in peers[1:5]:
        echo(0, d)
    relay(0, 1)
    for d in peers[5:]:
        echo(0, d)
    relay(1, 1)
    echo(1, peers[0])
    echo(1, peers[1])
    echo(1, peers[2])
    relay(0, 2)
    echo(1, peers[3])
    echo(1, peers[4])
    relay(1, 2)
    echo(1, peers[5])
    echo(1, peers[6])
    relay(0, 3)
    relay(1, 3)
    relay(0, 4)
    relay(1, 4)
    for g in range(2):
        for k in range(8):
            j = 2 * k + 1 - s
            arrived(xs.at[g, j], es.at[g, j], er.at[g, j])
    for n in range(18):
        if n < 2:
            ref = bank.at[1 - core, pl.ds(chunk(n, 0), 2)]
        else:
            hop, u, way = (n - 2) // 4 + 1, (n - 2) // 2 % 2, n % 2
            d = (-hop if way == 0 else hop) % 8
            start = chunk(u, d)
            ref = bank.at[1 - core, pl.ds(start + way, 1) if hop == 4 else pl.ds(start, 2)]
        arrived(ref, cs.at[n], cr.at[n])

    flip = 1.0 - 2.0 * s.astype(f32)
    response(bank, slabs, shifts, resp)
    for g in range(2):
        stage_j(xs.at[g], y, tab)
        stage_m(y, ahi, alo, tab)
        mid(ahi, alo, resp.at[g], mats)
        back(ahi, alo, q, mats)
        stage_k1(q, y, tab)
        stage_k0(y, out, tab, flip, g)
    result = pltpu.make_async_copy(out, out_h, loc.at[6])
    result.start()
    for c in sent:
        c.wait_send()
    result.wait()


def per_device(echoes, filters, slab_index, shifts):
    mats, tab = tables()
    hbm = pl.BlockSpec(memory_space=pl.ANY)
    smem = pl.BlockSpec(memory_space=pltpu.SMEM)
    dma = pltpu.SemaphoreType.DMA
    return pl.pallas_call(
        kernel,
        out_shape=jax.ShapeDtypeStruct((2, 16, N // 2), f32),
        in_specs=[hbm, hbm, smem, smem, hbm, hbm],
        out_specs=hbm,
        scratch_shapes=[
            pltpu.VMEM((2, 16, 2, 8, 2048), bf16),
            pltpu.VMEM((2, 8, 2, 8, 2048), bf16),
            pltpu.VMEM((2, 32, 256, 128), bf16),
            pltpu.VMEM((2, N), bf16),
            pltpu.VMEM((2, 256, 128), f32),
            pltpu.VMEM((2, 256, 128), f32),
            pltpu.VMEM((4, 256, 256), bf16),
            pltpu.VMEM((4, 256, 128), f32),
            pltpu.VMEM((2, 256, 8, 128), f32),
            pltpu.VMEM((2048, 256), bf16),
            pltpu.VMEM((2048, 256), bf16),
            pltpu.VMEM((2048, 256), f32),
            pltpu.VMEM((2, 2, 2048, 128), f32),
            pltpu.VMEM((2, 16, N // 2), f32),
            dma((24,)),
            dma((2, 16)),
            dma((2, 16)),
            dma((2,)),
            dma((2,)),
            dma((2, 4, 2)),
            dma((2, 4, 2)),
            dma((18,)),
            dma((18,)),
        ],
        compiler_params=pltpu.CompilerParams(
            collective_id=0, has_side_effects=True, vmem_limit_bytes=60 << 20
        ),
    )(
        echoes.reshape(2, 8, 2, 8, 2048), filters, slab_index, shifts,
        jnp.asarray(mats), jnp.asarray(tab),
    )


def solution(mesh):
    in_specs = (
        P(None, "blk", ("turn", "strip")),
        P(None, "blk", None),
        P(("blk", "turn")),
        P(("blk", "turn")),
    )
    out_specs = P(None, ("blk", "turn"), "strip")
    return jax.shard_map(
        per_device, mesh=mesh, in_specs=in_specs, out_specs=out_specs, check_vma=False
    )
```

profile of v0, /device:TPU:53, one launch (start us, length us, event | category | flops | bytes accessed | tf_op | source)
XLA Modules:
  0.0 69.5 jit_solution(6402930859924082127)
XLA Ops:
  0.0 66.4 %shard_map.64 = f32[2,16,16384]{2,1,0:T(8,128)} custom-call(bf16[2,8,2,8,2048]{4,3,2,1,0:T(8,128)(2,1)} %bitcast.1, bf16[2,2,32768]{2,1,0:T(2,128)(2,1)} %filters.1, s32[16]{0:T(128)} %slabs.1, s32[16]{0:T(128)} %shifts.1, bf16[4,256,256]{2,1,0:T(8,128)(2,1)} %constant.4.clone.mats_h, f32[4,256,128]{2,1,0:T(8,128)} %constant.5.clone.tab_h), custom_call_target="tpu_custom_call" | custom-call | tf_op jit(solution)/shard_map/pallas_call | solution.py:384
  66.4 3.0 %copy.8 = f32[2,16,16384]{2,1,0:T(8,128)} copy(f32[2,16,16384]{2,1,0:T(8,128)} %shard_map.64) | data formatting | bytes 4194304
where the time goes:
time: 69.6 us; the launch traced here: 69.5 us
  Pallas kernels  66.4 us (95%)
  local copies, waits for them, and re-layouts  3.05 us (4%)
    pallas_call x1, Pallas kernels, per_device(): pl.pallas_call(kernel, out_shape=jax.ShapeDtypeStruct((2, 16, N // 2), f3...  66.4 us
    unnamed x1, local copies, waits for them, and re-layouts  3.05 us

commit v1 on v0

--- a/solution.py
+++ b/solution.py
@@ -117,6 +117,24 @@
 def dot3(hi, lo, whi, wlo):
     d = functools.partial(jnp.dot, preferred_element_type=f32)
     return d(hi, whi) + d(lo, whi) + d(hi, wlo)
+
+def ahead(hi_ref, lo_ref, q, mats, chunk=512):
+    def body(i, _):
+        rows = pl.ds(pl.multiple_of(i * chunk, chunk), chunk)
+        q[rows, :] = dot3(hi_ref[rows, :], lo_ref[rows, :], mats[0], mats[1])
+        return 0
+    lax.fori_loop(0, 2048 // chunk, body, 0)
+
+def weigh(q, hi_ref, lo_ref, resp, chunk=128):
+    def body(i, _):
+        rows = pl.ds(pl.multiple_of(i * chunk, chunk), chunk)
+        p = cmul((q[rows, 0:128], q[rows, 128:256]), resp[0, rows, :], resp[1, rows, :])
+        for part, lanes in ((0, slice(0, 128)), (1, slice(128, 256))):
+            hi, lo = split(p[part])
+            hi_ref[rows, lanes] = hi
+            lo_ref[rows, lanes] = lo
+        return 0
+    lax.fori_loop(0, 2048 // chunk, body, 0)
 
 def mid(hi_ref, lo_ref, resp, mats, chunk=512):
     def body(i, _):
@@ -170,10 +188,10 @@
     ang = idx.astype(f32) * (2 * math.pi / N)
     return jnp.cos(ang), -jnp.sin(ang)
 
-def response(bank, slabs, shifts, resp):
+def response(bank, slabs, shifts, resp, groups):
     sub = lax.broadcasted_iota(jnp.int32, (8, 128), 0)
     lane = lax.broadcasted_iota(jnp.int32, (8, 128), 1)
-    for g in range(2):
+    for g in groups:
         def body(r, _):
             sl = slabs[8 * g + r]
             sh = shifts[8 * g + r]
@@ -211,8 +229,8 @@
 
 
 def kernel(
-    echoes, filters, slabs, shifts, mats_h, tab_h, out_h,
-    xs, est, bank, raw, lines, turned, mats, tab, y, ahi, alo, q, resp, out,
+    echoes, filters, slabs, shifts, mats_h, tab_h, out,
+    xs, est, bank, raw, lines, turned, mats, tab, y, ahi, alo, q, resp,
     loc, es, er, fs, fr, zs, zr, cs, cr,
 ):
     t, b, s = (lax.axis_index(n) for n in ("turn", "blk", "strip"))
@@ -281,99 +299,104 @@
         arrived(xs.at[g, j], es.at[g, j], er.at[g, j])
         forward(g, j)
 
-    def chunk(u, d):
-        side = xlo if u == 0 else 1 - xlo
-        return 2 * (side * 8 + (z + d) % 8)
-
-    def piece(u, d, hop, way):
-        start = chunk(u, d)
-        if hop == 4:
-            return bank.at[core, pl.ds(start + way, 1)]
-        return bank.at[core, pl.ds(start, 2)]
-
-    def over_z(u, hop, way):
-        d = (1 - hop) if way == 0 else (hop - 1)
-        ref = piece(u, d % 8, hop, way)
-        send(ref, ref, zs.at[way, hop - 1, u], zr.at[way, hop - 1, u], at_z(1 if way == 0 else 7))
-
-    def over_core(ref, n):
-        send(ref, ref, cs.at[n], cr.at[n], mate)
+    def slab(part, n, d):
+        side = xlo if n < 2 else 1 - xlo
+        return bank.at[part, 2 * (side * 8 + (z + d) % 8) + n % 2]
+
+    def over_z(n, hop, way):
+        ref = slab(core, n, (1 - hop if way == 0 else hop - 1) % 8)
+        send(ref, ref, zs.at[way, hop - 1, n], zr.at[way, hop - 1, n], at_z(1 if way == 0 else 7))
+
+    def over_core(n, d):
+        ref = slab(core, n, d)
+        send(ref, ref, cs.at[n, d], cr.at[n, d], mate)
 
     def relay(u, hop):
-        for way in range(2):
-            d = (-hop if way == 0 else hop) % 8
-            ref = piece(u, d, hop, way)
-            arrived(ref, zs.at[way, hop - 1, u], zr.at[way, hop - 1, u])
-            if hop < 4:
-                over_z(u, hop + 1, way)
-            n = 2 + (hop - 1) * 4 + 2 * u + way
-            over_core(ref, n)
-
-    own = bank.at[core, pl.ds(2 * b, 2)]
-    for i, d in ((0, 1), (1, 3)):
-        ref = bank.at[core, pl.ds(2 * b + i, 1)]
-        send(ref, ref, fs.at[i], fr.at[i], at_x(d))
-    over_z(0, 1, 0)
-    over_z(0, 1, 1)
-    for g in range(2):
+        for i in range(2):
+            n = 2 * u + i
+            for way in range(2):
+                if hop == 4 and way != i:
+                    continue
+                d = (-hop if way == 0 else hop) % 8
+                arrived(slab(core, n, d), zs.at[way, hop - 1, n], zr.at[way, hop - 1, n])
+                if hop < 3 or (hop == 3 and way == i):
+                    over_z(n, hop + 1, way)
+                over_core(n, d)
+
+    def own_filters():
+        for i, d in ((0, 1), (1, 3)):
+            ref = slab(core, i, 0)
+            send(ref, ref, fs.at[i], fr.at[i], at_x(d))
+        for i in range(2):
+            over_z(i, 1, 0)
+            over_z(i, 1, 1)
+
+    def other_filters():
+        for i in range(2):
+            arrived(slab(core, 2 + i, 0), fs.at[i], fr.at[i])
+            over_z(2 + i, 1, 0)
+            over_z(2 + i, 1, 1)
+            over_core(2 + i, 0)
+
+    def over_y(g):
         for k, d in enumerate(peers):
             send(est.at[:, d[0], g], xs.at[g, mine], loc.at[8 + 8 * g + k], er.at[g, mine], d)
-        forward(g, mine)
-    over_core(own, 0)
-
-    echo(0, peers[0])
-    for i in range(2):
-        arrived(bank.at[core, pl.ds(chunk(1, 0) + i, 1)], fs.at[i], fr.at[i])
-    over_z(1, 1, 0)
-    over_z(1, 1, 1)
-    over_core(bank.at[core, pl.ds(chunk(1, 0), 2)], 1)
-    for d in peers[1:5]:
-        echo(0, d)
-    relay(0, 1)
-    for d in peers[5:]:
-        echo(0, d)
-    relay(1, 1)
-    echo(1, peers[0])
-    echo(1, peers[1])
-    echo(1, peers[2])
-    relay(0, 2)
-    echo(1, peers[3])
-    echo(1, peers[4])
-    relay(1, 2)
-    echo(1, peers[5])
-    echo(1, peers[6])
-    relay(0, 3)
-    relay(1, 3)
-    relay(0, 4)
-    relay(1, 4)
-    for g in range(2):
+
+    def echoes_in(g):
         for k in range(8):
             j = 2 * k + 1 - s
             arrived(xs.at[g, j], es.at[g, j], er.at[g, j])
-    for n in range(18):
-        if n < 2:
-            ref = bank.at[1 - core, pl.ds(chunk(n, 0), 2)]
-        else:
-            hop, u, way = (n - 2) // 4 + 1, (n - 2) // 2 % 2, n % 2
-            d = (-hop if way == 0 else hop) % 8
-            start = chunk(u, d)
-            ref = bank.at[1 - core, pl.ds(start + way, 1) if hop == 4 else pl.ds(start, 2)]
-        arrived(ref, cs.at[n], cr.at[n])
+
+    def filters_in():
+        for n in range(4):
+            for d in range(8):
+                arrived(slab(1 - core, n, d), cs.at[n, d], cr.at[n, d])
 
     flip = 1.0 - 2.0 * s.astype(f32)
-    response(bank, slabs, shifts, resp)
-    for g in range(2):
-        stage_j(xs.at[g], y, tab)
-        stage_m(y, ahi, alo, tab)
-        mid(ahi, alo, resp.at[g], mats)
-        back(ahi, alo, q, mats)
-        stage_k1(q, y, tab)
-        stage_k0(y, out, tab, flip, g)
-    result = pltpu.make_async_copy(out, out_h, loc.at[6])
-    result.start()
+
+    own_filters()
+    forward(0, mine)
+    over_y(0)
+    for i in range(2): over_core(i, 0)
+    echo(0, peers[0])
+    other_filters()
+    for d in peers[1:3]: echo(0, d)
+    relay(0, 1)
+    for d in peers[3:5]: echo(0, d)
+    relay(1, 1)
+    forward(1, mine)
+    over_y(1)
+    for d in peers[5:]: echo(0, d)
+    echo(1, peers[0])
+    relay(0, 2)
+    for d in peers[1:3]: echo(1, d)
+    relay(1, 2)
+    for d in peers[3:5]: echo(1, d)
+    for d in peers[5:]: echo(1, d)
+    relay(0, 3)
+    echoes_in(0)
+    stage_j(xs.at[0], y, tab)
+    relay(1, 3)
+    stage_m(y, ahi, alo, tab)
+    relay(0, 4)
+    ahead(ahi, alo, q, mats)
+    relay(1, 4)
+    filters_in()
+    response(bank, slabs, shifts, resp, (0, 1))
+    weigh(q, ahi, alo, resp.at[0])
+    back(ahi, alo, q, mats)
+    stage_k1(q, y, tab)
+    stage_k0(y, out, tab, flip, 0)
+    echoes_in(1)
+    stage_j(xs.at[1], y, tab)
+    stage_m(y, ahi, alo, tab)
+    ahead(ahi, alo, q, mats)
+    weigh(q, ahi, alo, resp.at[1])
+    back(ahi, alo, q, mats)
+    stage_k1(q, y, tab)
+    stage_k0(y, out, tab, flip, 1)
     for c in sent:
         c.wait_send()
-    result.wait()
 
 
 def per_device(echoes, filters, slab_index, shifts):
@@ -383,9 +406,9 @@
     dma = pltpu.SemaphoreType.DMA
     return pl.pallas_call(
         kernel,
-        out_shape=jax.ShapeDtypeStruct((2, 16, N // 2), f32),
+        out_shape=pltpu.VMEM((2, 16, N // 2), f32),
         in_specs=[hbm, hbm, smem, smem, hbm, hbm],
-        out_specs=hbm,
+        out_specs=pl.BlockSpec(memory_space=pltpu.VMEM),
         scratch_shapes=[
             pltpu.VMEM((2, 16, 2, 8, 2048), bf16),
             pltpu.VMEM((2, 8, 2, 8, 2048), bf16),
@@ -400,19 +423,18 @@
             pltpu.VMEM((2048, 256), bf16),
             pltpu.VMEM((2048, 256), f32),
             pltpu.VMEM((2, 2, 2048, 128), f32),
-            pltpu.VMEM((2, 16, N // 2), f32),
             dma((24,)),
             dma((2, 16)),
             dma((2, 16)),
             dma((2,)),
             dma((2,)),
-            dma((2, 4, 2)),
-            dma((2, 4, 2)),
-            dma((18,)),
-            dma((18,)),
+            dma((2, 4, 4)),
+            dma((2, 4, 4)),
+            dma((4, 8)),
+            dma((4, 8)),
         ],
         compiler_params=pltpu.CompilerParams(
-            collective_id=0, has_side_effects=True, vmem_limit_bytes=60 << 20
+            collective_id=0, has_side_effects=True, vmem_limit_bytes=64946176
         ),
     )(
         echoes.reshape(2, 8, 2, 8, 2048), filters, slab_index, shifts,

time: 69.6 us -> 51.8 us (0.74)
  the two profiles are of different devices: /device:TPU:53 before, /device:TPU:1 now
where the time goes in v1:
time: 51.8 us; the launch traced here: 51.7 us
  Pallas kernels  50.4 us (97%)
  local copies, waits for them, and re-layouts  1.32 us (3%)
    pallas_call x1, Pallas kernels, per_device(): pl.pallas_call(kernel, out_shape=pltpu.VMEM((2, 16, N // 2), f32), in_spe...  50.4 us
    unnamed x1, local copies, waits for them, and re-layouts  1.32 us

profile of v1, /device:TPU:1, one launch (start us, length us, event | category | flops | bytes accessed | tf_op | source)
XLA Modules:
  0.0 51.7 jit_solution(12898433102623790763)
XLA Ops:
  0.0 50.4 %shard_map.64 = f32[2,16,16384]{2,1,0:T(8,128)S(1)} custom-call(bf16[2,8,2,8,2048]{4,3,2,1,0:T(8,128)(2,1)} %bitcast.1, bf16[2,2,32768]{2,1,0:T(2,128)(2,1)} %filters.1, s32[16]{0:T(128)} %slabs.1, s32[16]{0:T(128)} %shifts.1, bf16[4,256,256]{2,1,0:T(8,128)(2,1)} %constant.4.clone.mats_h, f32[4,256,128]{2,1,0:T(8,128)} %constant.5.clone.tab_h), custom_call_target="tpu_custom_call" | custom-call | tf_op jit(solution)/shard_map/pallas_call | solution.py:407
  50.4 1.3 %copy.8 = f32[2,16,16384]{2,1,0:T(8,128)} copy(f32[2,16,16384]{2,1,0:T(8,128)S(1)} %shard_map.64) | data formatting | bytes 4194304

commit v2 on v1

--- a/solution.py
+++ b/solution.py
@@ -118,54 +118,30 @@
     d = functools.partial(jnp.dot, preferred_element_type=f32)
     return d(hi, whi) + d(lo, whi) + d(hi, wlo)
 
-def ahead(hi_ref, lo_ref, q, mats, chunk=512):
+def ahead_part(i, hi_ref, lo_ref, q, mats, chunk):
+    rows = pl.ds(pl.multiple_of(i * chunk, chunk), chunk)
+    q[rows, :] = dot3(hi_ref[rows, :], lo_ref[rows, :], mats[0], mats[1])
+
+def ahead(hi_ref, lo_ref, q, mats, chunk=1024):
     def body(i, _):
-        rows = pl.ds(pl.multiple_of(i * chunk, chunk), chunk)
-        q[rows, :] = dot3(hi_ref[rows, :], lo_ref[rows, :], mats[0], mats[1])
+        ahead_part(i, hi_ref, lo_ref, q, mats, chunk)
         return 0
     lax.fori_loop(0, 2048 // chunk, body, 0)
 
-def weigh(q, hi_ref, lo_ref, resp, chunk=128):
-    def body(i, _):
-        rows = pl.ds(pl.multiple_of(i * chunk, chunk), chunk)
-        p = cmul((q[rows, 0:128], q[rows, 128:256]), resp[0, rows, :], resp[1, rows, :])
-        for part, lanes in ((0, slice(0, 128)), (1, slice(128, 256))):
-            hi, lo = split(p[part])
-            hi_ref[rows, lanes] = hi
-            lo_ref[rows, lanes] = lo
-        return 0
-    lax.fori_loop(0, 2048 // chunk, body, 0)
-
-def mid(hi_ref, lo_ref, resp, mats, chunk=512):
-    def body(i, _):
-        rows = pl.ds(pl.multiple_of(i * chunk, chunk), chunk)
-        s = dot3(hi_ref[rows, :], lo_ref[rows, :], mats[0], mats[1])
-        p = cmul((s[:, :128], s[:, 128:]), resp[0, rows, :], resp[1, rows, :])
-        for part, lanes in ((0, slice(0, 128)), (1, slice(128, 256))):
-            hi, lo = split(p[part])
-            hi_ref[rows, lanes] = hi
-            lo_ref[rows, lanes] = lo
-        return 0
-    lax.fori_loop(0, 2048 // chunk, body, 0)
-
-def back(hi_ref, lo_ref, q, mats, chunk=512):
-    def body(i, _):
-        rows = pl.ds(pl.multiple_of(i * chunk, chunk), chunk)
-        q[rows, :] = dot3(hi_ref[rows, :], lo_ref[rows, :], mats[2], mats[3])
-        return 0
-    lax.fori_loop(0, 2048 // chunk, body, 0)
-
-def stage_k1(q, y, tab):
-    def body(k0, _):
-        v = []
-        for k1 in range(16):
-            rows = pl.ds(pl.multiple_of(k0 * 128 + k1 * 8, 8), 8)
-            row = pl.ds(k0 + 16 * k1, 1)
-            v.append(cmulc((q[rows, 0:128], q[rows, 128:256]), tab[0, row, :], tab[1, row, :]))
-        for m1, a in enumerate(dft16(v, 1)):
-            y[0, k0 * 16 + m1], y[1, k0 * 16 + m1] = a
-        return 0
-    lax.fori_loop(0, 16, body, 0)
+def weigh_back(i, q, resp, mats, chunk):
+    rows = pl.ds(pl.multiple_of(i * chunk, chunk), chunk)
+    p = cmul((q[rows, 0:128], q[rows, 128:256]), resp[0, rows, :], resp[1, rows, :])
+    hi, lo = split(jnp.concatenate(p, axis=1))
+    q[rows, :] = dot3(hi, lo, mats[2], mats[3])
+
+def stage_k1(k0, q, y, tab):
+    v = []
+    for k1 in range(16):
+        rows = pl.ds(pl.multiple_of(k0 * 128 + k1 * 8, 8), 8)
+        row = pl.ds(k0 + 16 * k1, 1)
+        v.append(cmulc((q[rows, 0:128], q[rows, 128:256]), tab[0, row, :], tab[1, row, :]))
+    for m1, a in enumerate(dft16(v, 1)):
+        y[0, k0 * 16 + m1], y[1, k0 * 16 + m1] = a
 
 def stage_k0(y, out, tab, flip, g):
     def body(m1, _):
@@ -178,7 +154,8 @@
             v.append(a)
         for j, a in enumerate(half16(v, 1, flip)):
             lanes = pl.ds(pl.multiple_of(j * 2048 + m1 * 128, 128), 128)
-            out[0, 8 * g:8 * g + 8, lanes], out[1, 8 * g:8 * g + 8, lanes] = a
+            rows = pl.ds(pl.multiple_of(8 * g, 8), 8)
+            out[0, rows, lanes], out[1, rows, lanes] = a
         return 0
     lax.fori_loop(0, 16, body, 0)
 
@@ -188,27 +165,22 @@
     ang = idx.astype(f32) * (2 * math.pi / N)
     return jnp.cos(ang), -jnp.sin(ang)
 
-def response(bank, slabs, shifts, resp, groups):
+def response(line, r, bank, slabs, shifts, resp):
     sub = lax.broadcasted_iota(jnp.int32, (8, 128), 0)
     lane = lax.broadcasted_iota(jnp.int32, (8, 128), 1)
-    for g in groups:
-        def body(r, _):
-            sl = slabs[8 * g + r]
-            sh = shifts[8 * g + r]
-            e = [phase((16 * (sub + 8 * h) + 256 * lane) * sh) for h in range(2)]
-            w = phase(jnp.full((8, 128), 1, jnp.int32) * sh)
-            for i in range(16):
-                hr = bank[0, sl, 16 * i:16 * i + 16, :].astype(f32)
-                hi = bank[1, sl, 16 * i:16 * i + 16, :].astype(f32)
-                for h in range(2):
-                    o = cmul((hr[8 * h:8 * h + 8], hi[8 * h:8 * h + 8]), *e[h])
-                    rows = pl.ds((16 * i + 8 * h) * 8 + r, 8, stride=8)
-                    resp[g, 0, rows, :] = o[0]
-                    resp[g, 1, rows, :] = o[1]
-                if i < 15:
-                    e = [cmul(x, *w) for x in e]
-            return 0
-        lax.fori_loop(0, 8, body, 0)
+    sl, sh = slabs[line], shifts[line]
+    e = [phase((16 * (sub + 8 * h) + 256 * lane) * sh) for h in range(2)]
+    w = phase(jnp.full((8, 128), 1, jnp.int32) * sh)
+    for i in range(16):
+        hr = bank[0, sl, 16 * i:16 * i + 16, :].astype(f32)
+        hi = bank[1, sl, 16 * i:16 * i + 16, :].astype(f32)
+        for h in range(2):
+            o = cmul((hr[8 * h:8 * h + 8], hi[8 * h:8 * h + 8]), *e[h])
+            rows = pl.ds((16 * i + 8 * h) * 8 + r, 8, stride=8)
+            resp[0, rows, :] = o[0]
+            resp[1, rows, :] = o[1]
+        if i < 15:
+            e = [cmul(x, *w) for x in e]
 
 
 def place_filters(raw, lines, turned, bank, part, chunk):
@@ -230,7 +202,7 @@
 
 def kernel(
     echoes, filters, slabs, shifts, mats_h, tab_h, out,
-    xs, est, bank, raw, lines, turned, mats, tab, y, ahi, alo, q, resp,
+    xs, est, bank, raw, lines, turned, mats, tab, y, ahi, alo, q0, q1, resp0, resp1,
     loc, es, er, fs, fr, zs, zr, cs, cr,
 ):
     t, b, s = (lax.axis_index(n) for n in ("turn", "blk", "strip"))
@@ -374,26 +346,49 @@
     for d in peers[3:5]: echo(1, d)
     for d in peers[5:]: echo(1, d)
     relay(0, 3)
+
     echoes_in(0)
     stage_j(xs.at[0], y, tab)
     relay(1, 3)
     stage_m(y, ahi, alo, tab)
     relay(0, 4)
-    ahead(ahi, alo, q, mats)
+    ahead(ahi, alo, q0, mats)
     relay(1, 4)
-    filters_in()
-    response(bank, slabs, shifts, resp, (0, 1))
-    weigh(q, ahi, alo, resp.at[0])
-    back(ahi, alo, q, mats)
-    stage_k1(q, y, tab)
-    stage_k0(y, out, tab, flip, 0)
+
     echoes_in(1)
     stage_j(xs.at[1], y, tab)
     stage_m(y, ahi, alo, tab)
-    ahead(ahi, alo, q, mats)
-    weigh(q, ahi, alo, resp.at[1])
-    back(ahi, alo, q, mats)
-    stage_k1(q, y, tab)
+    filters_in()
+
+    def shape(i, _):
+        ahead_part(i, ahi, alo, q1, mats, 512)
+        for half in range(2):
+            response(2 * i + half, 2 * i + half, bank, slabs, shifts, resp0)
+            response(8 + 2 * i + half, 2 * i + half, bank, slabs, shifts, resp1)
+        return 0
+
+    lax.fori_loop(0, 4, shape, 0)
+
+    def first(i, _):
+        weigh_back(i, q0, resp0, mats, 512)
+        return 0
+
+    lax.fori_loop(0, 4, first, 0)
+
+    def second(i, _):
+        weigh_back(i, q1, resp1, mats, 512)
+        for n in range(4):
+            stage_k1(4 * i + n, q0, y, tab)
+        return 0
+
+    lax.fori_loop(0, 4, second, 0)
+    stage_k0(y, out, tab, flip, 0)
+
+    def last(k0, _):
+        stage_k1(k0, q1, y, tab)
+        return 0
+
+    lax.fori_loop(0, 16, last, 0)
     stage_k0(y, out, tab, flip, 1)
     for c in sent:
         c.wait_send()
@@ -422,7 +417,9 @@
             pltpu.VMEM((2048, 256), bf16),
             pltpu.VMEM((2048, 256), bf16),
             pltpu.VMEM((2048, 256), f32),
-            pltpu.VMEM((2, 2, 2048, 128), f32),
+            pltpu.VMEM((2048, 256), f32),
+            pltpu.VMEM((2, 2048, 128), f32),
+            pltpu.VMEM((2, 2048, 128), f32),
             dma((24,)),
             dma((2, 16)),
             dma((2, 16)),

time: 51.8 us -> 48.7 us (0.940)
  the two profiles are of different devices: /device:TPU:1 before, /device:TPU:16 now
where the time goes in v2:
time: 48.7 us; the launch traced here: 48.6 us
  Pallas kernels  47.2 us (97%)
  local copies, waits for them, and re-layouts  1.32 us (3%)
    pallas_call x1, Pallas kernels, per_device(): pl.pallas_call(kernel, out_shape=pltpu.VMEM((2, 16, N // 2), f32), in_spe...  47.2 us
    unnamed x1, local copies, waits for them, and re-layouts  1.32 us

profile of v2, /device:TPU:16, one launch (start us, length us, event | category | flops | bytes accessed | tf_op | source)
XLA Modules:
  0.0 48.6 jit_solution(15011061544224081172)
XLA Ops:
  0.0 47.2 %shard_map.64 = f32[2,16,16384]{2,1,0:T(8,128)S(1)} custom-call(bf16[2,8,2,8,2048]{4,3,2,1,0:T(8,128)(2,1)} %bitcast.1, bf16[2,2,32768]{2,1,0:T(2,128)(2,1)} %filters.1, s32[16]{0:T(128)} %slabs.1, s32[16]{0:T(128)} %shifts.1, bf16[4,256,256]{2,1,0:T(8,128)(2,1)} %constant.4.clone.mats_h, f32[4,256,128]{2,1,0:T(8,128)} %constant.5.clone.tab_h), custom_call_target="tpu_custom_call" | custom-call | tf_op jit(solution)/shard_map/pallas_call | solution.py:402
  47.2 1.3 %copy.8 = f32[2,16,16384]{2,1,0:T(8,128)} copy(f32[2,16,16384]{2,1,0:T(8,128)S(1)} %shard_map.64) | data formatting | bytes 4194304

commit v3 on v2

--- a/solution.py
+++ b/solution.py
@@ -331,12 +331,12 @@
     over_y(0)
     for i in range(2): over_core(i, 0)
     echo(0, peers[0])
+    forward(1, mine)
     other_filters()
     for d in peers[1:3]: echo(0, d)
     relay(0, 1)
     for d in peers[3:5]: echo(0, d)
     relay(1, 1)
-    forward(1, mine)
     over_y(1)
     for d in peers[5:]: echo(0, d)
     echo(1, peers[0])
@@ -370,10 +370,10 @@
     lax.fori_loop(0, 4, shape, 0)
 
     def first(i, _):
-        weigh_back(i, q0, resp0, mats, 512)
-        return 0
-
-    lax.fori_loop(0, 4, first, 0)
+        weigh_back(i, q0, resp0, mats, 1024)
+        return 0
+
+    lax.fori_loop(0, 2, first, 0)
 
     def second(i, _):
         weigh_back(i, q1, resp1, mats, 512)

time: 48.7 us -> 52.7 us (1.082)
  Pallas kernels: 47.2 us -> 51.1 us
    pallas_call x1, Pallas kernels: 47.2 us -> 51.1 us  [per_device(): pl.pallas_call(kernel, out_shape=pltpu.VMEM((2, 16, N // 2), f32), in_spe...]
where the time goes in v3:
time: 52.7 us; the launch traced here: 52.4 us
  Pallas kernels  51.1 us (97%)
  local copies, waits for them, and re-layouts  1.32 us (3%)
    pallas_call x1, Pallas kernels, per_device(): pl.pallas_call(kernel, out_shape=pltpu.VMEM((2, 16, N // 2), f32), in_spe...  51.1 us
    unnamed x1, local copies, waits for them, and re-layouts  1.32 us

profile of v3, /device:TPU:16, one launch (start us, length us, event | category | flops | bytes accessed | tf_op | source)
XLA Modules:
  0.0 52.4 jit_solution(7916195536699537)
XLA Ops:
  0.0 51.1 %shard_map.64 = f32[2,16,16384]{2,1,0:T(8,128)S(1)} custom-call(bf16[2,8,2,8,2048]{4,3,2,1,0:T(8,128)(2,1)} %bitcast.1, bf16[2,2,32768]{2,1,0:T(2,128)(2,1)} %filters.1, s32[16]{0:T(128)} %slabs.1, s32[16]{0:T(128)} %shifts.1, bf16[4,256,256]{2,1,0:T(8,128)(2,1)} %constant.4.clone.mats_h, f32[4,256,128]{2,1,0:T(8,128)} %constant.5.clone.tab_h), custom_call_target="tpu_custom_call" | custom-call | tf_op jit(solution)/shard_map/pallas_call | solution.py:402
  51.1 1.3 %copy.8 = f32[2,16,16384]{2,1,0:T(8,128)} copy(f32[2,16,16384]{2,1,0:T(8,128)S(1)} %shard_map.64) | data formatting | bytes 4194304

commit v4 on v2

--- a/solution.py
+++ b/solution.py
@@ -336,9 +336,9 @@
     relay(0, 1)
     for d in peers[3:5]: echo(0, d)
     relay(1, 1)
+    for d in peers[5:]: echo(0, d)
     forward(1, mine)
     over_y(1)
-    for d in peers[5:]: echo(0, d)
     echo(1, peers[0])
     relay(0, 2)
     for d in peers[1:3]: echo(1, d)

time: 48.7 us -> 48.7 us (level)
  no operation moved by 1% of the time
where the time goes in v4:
time: 48.7 us; the launch traced here: 48.6 us
  Pallas kernels  47.2 us (97%)
  local copies, waits for them, and re-layouts  1.32 us (3%)
    pallas_call x1, Pallas kernels, per_device(): pl.pallas_call(kernel, out_shape=pltpu.VMEM((2, 16, N // 2), f32), in_spe...  47.2 us
    unnamed x1, local copies, waits for them, and re-layouts  1.32 us

profile of v4, /device:TPU:16, one launch (start us, length us, event | category | flops | bytes accessed | tf_op | source)
XLA Modules:
  0.0 48.6 jit_solution(1645386312917422321)
XLA Ops:
  0.0 47.2 %shard_map.64 = f32[2,16,16384]{2,1,0:T(8,128)S(1)} custom-call(bf16[2,8,2,8,2048]{4,3,2,1,0:T(8,128)(2,1)} %bitcast.1, bf16[2,2,32768]{2,1,0:T(2,128)(2,1)} %filters.1, s32[16]{0:T(128)} %slabs.1, s32[16]{0:T(128)} %shifts.1, bf16[4,256,256]{2,1,0:T(8,128)(2,1)} %constant.4.clone.mats_h, f32[4,256,128]{2,1,0:T(8,128)} %constant.5.clone.tab_h), custom_call_target="tpu_custom_call" | custom-call | tf_op jit(solution)/shard_map/pallas_call | solution.py:402
  47.2 1.3 %copy.8 = f32[2,16,16384]{2,1,0:T(8,128)} copy(f32[2,16,16384]{2,1,0:T(8,128)S(1)} %shard_map.64) | data formatting | bytes 4194304
